TPU v7x, 256 devices: a whole 4x4x8 slice. The times are simulated.
256 devices in a mesh: vrow: 32 (over z, y), vcol: 8 (over x, core).
Axes of the slice: x: 4, y: 4, z: 8, core: 2. Of those that a mesh axis runs over, the one named last changes fastest.
Arguments:
- policy_hidden: bfloat16 [1024, 3584], P(None, 'vcol'), may hold values from -400 to 400
- ref_hidden: bfloat16 [1024, 3584], P(None, 'vcol'), may hold values from -400 to 400
- mix_num: int32 [1024], replicated, may hold values from 0 to 16, as said below
- mix_den: int32 [1024], replicated, may hold values from 2 to 16
- policy_unembed: bfloat16 [3584, 131072], P(None, ('vrow', 'vcol')), may hold values from -0.09375 to 0.09375
- ref_unembed: bfloat16 [3584, 131072], P(None, ('vrow', 'vcol')), may hold values from -0.09375 to 0.09375
Outputs:
- mix_logprobs: float32 [1024, 131072], P(None, ('vrow', 'vcol'))
Inputs may be any that keep to these rules, and one draw needn't show every extreme that they name: Each sequence's mix_num is at most its mix_den.
All inputs are finite; a program needn't handle non-finite values.
Results may differ from a plain program's by a relative error of at most 0.0003.
Values may be sent and summed in bfloat16 or wider, within the bound.
A program may use at most 64 MiB of HBM per device.

v0:
```python
import jax
import jax.numpy as jnp
from jax import lax
from jax.sharding import Mesh
from jax.sharding import PartitionSpec as P

VCOL = ("vcol_0", "vcol_1")
VROW_VCOL = ("vrow_0", "vrow_1", "vcol_0", "vcol_1")


def rows_first(arrays, axis, dims):
    turned = [jnp.moveaxis(a, dim, 0) for a, dim in zip(arrays, dims)]
    both = jnp.concatenate([t.reshape(len(t), -1) for t in turned], axis=1)
    filled, at, done = (lax.all_gather(both, axis, axis=0, tiled=True), 0, [])
    for t, dim in zip(turned, dims):
        slab = filled[:, at : at + t[0].size].reshape(-1, *t.shape[1:])
        done.append(jnp.moveaxis(slab, 0, dim))
        at += t[0].size
    return tuple(done)


def collected_together(value, axis):
    leaves = jax.tree.leaves(value)
    order = sorted(range(len(leaves)), key=lambda k: -leaves[k].size)
    width = (1, *leaves[order[0]].shape)[-1]
    lines = [
        jnp.pad(leaves[k].reshape(-1), (0, -leaves[k].size % width)).reshape(-1, width)
        for k in order
    ]
    both, at, found = (lax.all_gather(jnp.concatenate(lines), axis), 0, {})
    for k, line in zip(order, lines):
        slab = both[:, at : at + len(line)].reshape(len(both), -1)
        found[k] = slab[:, : leaves[k].size].reshape(-1, *leaves[k].shape)
        at += len(line)
    numbers = iter(range(len(leaves)))
    return jax.tree.map(lambda _: found[next(numbers)], value)


def joined_all(value, axes, combine):
    for axis in axes:
        pieces = collected_together(value, axis)
        value = jax.tree.map(lambda part: part[0], pieces)
        for k in range(1, lax.axis_size(axis)):
            value = combine(value, jax.tree.map(lambda part: part[k], pieces))
    return value


def combine_stats(first, second):
    high = jnp.maximum(first[0], second[0])
    total = first[1] * jnp.exp(first[0] - high) + second[1] * jnp.exp(second[0] - high)
    return (high, total)


def body(policy_hidden, ref_hidden, mix_num, mix_den, policy_unembed, ref_unembed):
    policy_full, ref_full = rows_first((policy_hidden, ref_hidden), VCOL, (1, 1))
    policy_logits = jnp.dot(policy_full, policy_unembed, preferred_element_type=jnp.float32)
    ref_logits = jnp.dot(ref_full, ref_unembed, preferred_element_type=jnp.float32)
    beta = (mix_num.astype(jnp.float32) / mix_den.astype(jnp.float32))[:, None]
    mixed = (1.0 - beta) * policy_logits + beta * ref_logits
    local_top = jnp.max(mixed, axis=1, keepdims=True)
    local_total = jnp.sum(jnp.exp(mixed - local_top), axis=1, keepdims=True)
    top, total = joined_all((local_top, local_total), VROW_VCOL, combine_stats)
    return mixed - top - jnp.log(total)


def solution(mesh):
    finer = Mesh(mesh.devices.reshape(8, 4, 4, 2), ("vrow_0", "vrow_1", "vcol_0", "vcol_1"))
    placed = (P(None, VCOL), P(None, VCOL), P(), P(), P(None, VROW_VCOL), P(None, VROW_VCOL))
    return jax.shard_map(
        body, mesh=finer, in_specs=placed, out_specs=P(None, VROW_VCOL), check_vma=False
    )
```

profile of v0, /device:TPU:1, one launch (start us, length us, event | category | flops | bytes accessed | tf_op | source)
XLA Modules:
  0.0 172.9 jit_solution(6092440054672598661)
XLA Ops:
  6.5 0.0 all-gather.6.cloned.1.call-start
  6.5 2.9 %pad_maximum_fusion = bf16[448,2048]{1,0:T(8,128)(2,1)} fusion(bf16[448,1024]{1,0:T(8,128)(2,1)} %bitcast.319, bf16[448,1024]{1,0:T(8,128)(2,1)} %bitcast.320), kind=kLoop, calls=%fused_computation.7 | loop fusion | flops 3670016 | bytes 3670016 | tf_op jit(solution)/shard_map/concatenate | solution.py:13
  9.4 0.0 all-gather.6.cloned.1.call-update
  9.5 0.0 copy-done
  9.5 0.0 copy-done.1
  9.5 82.9 %all-gather.6.cloned.1.call-done = bf16[3584,2048]{1,0:T(8,128)(2,1)} async-done(((bf16[448,2048]{1,0:T(8,128)(2,1)}), bf16[3584,2048]{1,0:T(8,128)(2,1)}) %all-gather.6.cloned.1.call-update) | async-done | bytes 14680080 | tf_op jit(solution)/shard_map/all_gather | solution.py:14
  92.4 7.5 %fusion = f32[1024,512]{0,1:T(8,128)S(1)} fusion(bf16[3584,512]{1,0:T(8,128)(2,1)} %param.11, bf16[3584,2048]{1,0:T(8,128)(2,1)} %all-gather.6.cloned.1.call-done), kind=kOutput, calls=%fused_computation | convolution fusion | flops 3758096384 | bytes 13107200 | tf_op jit(solution)/shard_map/dot_general | solution.py:57
  100.0 0.8 copy-done.2
  100.8 1.0 copy-done.3
  101.9 4.1 %fusion.62 = (f32[1024]{0:T(1024)S(1)}, f32[1024,512]{0,1:T(8,128)S(1)}) fusion(f32[1024,512]{0,1:T(8,128)S(1)} %fusion, f32[1024]{0:T(1024)S(1)} %get-tuple-element.14, bf16[3584,512]{1,0:T(8,128)(2,1)S(1)} %copy-done.3, bf16[3584,2048]{1,0:T(8,128)(2,1)S(1)} %copy-done.2, f32[1024]{0:T(1024)S(1)} %get-tuple-element.13), kind=kOutput, calls=%fused_computation.100 | convolution fusion | flops 3760192512 | bytes 15216640 | tf_op jit(solution)/shard_map/dot_general | solution.py:56
  106.0 0.3 exponential_reduce_fusion
  106.3 19.7 %all-gather = f32[16384,1]{0,1:T(1,128)S(1)} all-gather(f32[2048,1]{0,1:T(1,128)S(1)} %pad_maximum_fusion.1), channel_id=2, replica_groups=mesh['vrow_0'=8,'vrow_1'=4,'vcol_0'=4,'vcol_1'=2] {'vrow_0'}, dimensions={0}, use_global_device_ids=true | all-gather | bytes 73728 | tf_op jit(solution)/shard_map/all_gather | solution.py:30
  126.1 0.1 fusion.25
  126.2 9.5 %all-gather.1 = f32[8192,1]{0,1:T(1,128)S(1)} all-gather(f32[2048,1]{0,1:T(1,128)S(1)} %pad_maximum_fusion.2), channel_id=3, replica_groups=mesh['vrow_0'=8,'vrow_1'=4,'vcol_0'=4,'vcol_1'=2] {'vrow_1'}, dimensions={0}, use_global_device_ids=true | all-gather | bytes 40960 | tf_op jit(solution)/shard_map/all_gather | solution.py:30
  135.7 0.5 broadcast.16
  136.2 0.7 reduce.12
  137.0 0.1 fusion.16
  137.1 9.0 %all-gather.2 = f32[8192,1]{0,1:T(1,128)S(1)} all-gather(f32[2048,1]{0,1:T(1,128)S(1)} %pad_maximum_fusion.3), channel_id=4, replica_groups=mesh['vrow_0'=8,'vrow_1'=4,'vcol_0'=4,'vcol_1'=2] {'vcol_0'}, dimensions={0}, use_global_device_ids=true | all-gather | bytes 40960 | tf_op jit(solution)/shard_map/all_gather | solution.py:30
  146.1 0.7 reduce.13
  146.9 0.1 fusion.7
  146.9 13.7 %all-gather.3 = f32[4096,1]{0,1:T(1,128)S(1)} all-gather(f32[2048,1]{0,1:T(1,128)S(1)} %pad_maximum_fusion.4), channel_id=5, replica_groups=mesh['vrow_0'=8,'vrow_1'=4,'vcol_0'=4,'vcol_1'=2] {'vcol_1'}, dimensions={0}, use_global_device_ids=true | all-gather | bytes 24576 | tf_op jit(solution)/shard_map/all_gather | solution.py:30
  160.6 0.7 reduce.14
  161.4 1.8 %subtract_subtract_fusion = f32[1024,512]{0,1:T(8,128)} fusion(f32[1024,512]{0,1:T(8,128)S(1)} %get-tuple-element.20, f32[1024]{0:T(1024)S(1)} %get-tuple-element.5, f32[1024]{0:T(1024)S(1)} %get-tuple-element.6), kind=kLoop, calls=%fused_computation.4 | loop fusion | flops 1048576 | bytes 4202496 | tf_op jit(solution)/shard_map/sub | solution.py:63
  163.1 2.9 %copy.8 = f32[1024,512]{1,0:T(8,128)} copy(f32[1024,512]{0,1:T(8,128)} %subtract_subtract_fusion) | data formatting | bytes 4194304 | tf_op jit(solution)/shard_map/sub | solution.py:63
  (15 shorter events, 0.2 us)
Async XLA Ops:
  6.5 85.9 %all-gather.6.cloned.1.call-start = ((), (), s32[]{:S(2)}) async-start(), calls=%async_computation | async-start | bytes 16515072 | tf_op jit(solution)/shard_map/all_gather | solution.py:14
  6.5 2.9 %copy-start = (s32[1024]{0:T(1024)S(1)}, s32[1024]{0:T(1024)}, u32[]{:S(2)}) copy-start(s32[1024]{0:T(1024)} %param.9) | copy-start | bytes 12292
  6.5 2.9 %copy-start.1 = (s32[1024]{0:T(1024)S(1)}, s32[1024]{0:T(1024)}, u32[]{:S(2)}) copy-start(s32[1024]{0:T(1024)} %param.8) | copy-start | bytes 12292
  92.4 8.4 %copy-start.2 = (bf16[3584,2048]{1,0:T(8,128)(2,1)S(1)}, bf16[3584,2048]{1,0:T(8,128)(2,1)}, u32[]{:S(2)}) copy-start(bf16[3584,2048]{1,0:T(8,128)(2,1)} %all-gather.6.cloned.1.call-done) | copy-start | bytes 44040196
  92.4 9.4 %copy-start.3 = (bf16[3584,512]{1,0:T(8,128)(2,1)S(1)}, bf16[3584,512]{1,0:T(8,128)(2,1)}, u32[]{:S(2)}) copy-start(bf16[3584,512]{1,0:T(8,128)(2,1)} %param.10) | copy-start | bytes 11010052
Sparse Core Ops, SparseCore 0:
  9.6 82.7 all-gather.5
where the time goes:
time: 173 us
  waiting for transfers between devices  82.9 us (48%)
  blocking collectives  52 us (30%)
  between operations  13.5 us (8%)
  matrix products  11.7 us (7%)
  other arithmetic  7.39 us (4%)
  local copies, waits for them, and re-layouts  5.37 us (3%)
    all_gather x1, waiting for transfers between devices, rows_first(): filled, at, done = (lax.all_gather(both, axis, axis=0, tiled=True), 0, [])  82.9 us
    all_gather x4, blocking collectives, collected_together(): both, at, found = (lax.all_gather(jnp.concatenate(lines), axis), 0, {})  52 us
    dot_general x1, matrix products, body(): jnp.dot(ref_full, ref_unembed, preferred_element_type=jnp.float32)  7.54 us
    dot_general x1, matrix products, body(): jnp.dot(policy_full, policy_unembed, preferred_element_type=jnp.float32)  4.12 us
  transfers between devices with their start and end apart: 1, of which 1 were waited for; matrix products, arithmetic and copies ran while one was open for 0% of the time, Pallas kernels for 0%

commit v1 on v0

--- a/solution.py
+++ b/solution.py
@@ -11,7 +11,13 @@
 def rows_first(arrays, axis, dims):
     turned = [jnp.moveaxis(a, dim, 0) for a, dim in zip(arrays, dims)]
     both = jnp.concatenate([t.reshape(len(t), -1) for t in turned], axis=1)
-    filled, at, done = (lax.all_gather(both, axis, axis=0, tiled=True), 0, [])
+    filled, at, done = (
+        jnp.concatenate(
+            lax.all_to_all(jnp.stack([both] * lax.axis_size(axis)), axis, 0, 0), axis=0
+        ),
+        0,
+        [],
+    )
     for t, dim in zip(turned, dims):
         slab = filled[:, at : at + t[0].size].reshape(-1, *t.shape[1:])
         done.append(jnp.moveaxis(slab, 0, dim))

time: 173 us -> 253 us (1.46)
  waiting for transfers between devices: 82.9 us -> 161 us
  between operations: 13.5 us -> 0.15 us
  starting transfers between devices: 0.01 us -> 8.76 us
  local copies, waits for them, and re-layouts: 5.37 us -> 9.05 us
    all_to_all x0 -> x1, waiting for transfers between devices: none -> 161 us  [rows_first(): lax.all_to_all(jnp.stack([both] * lax.axis_size(axis)), axis, 0, 0)]
    all_gather x1 -> x0, waiting for transfers between devices: 82.9 us -> none  [rows_first(): filled, at, done = (lax.all_gather(both, axis, axis=0, tiled=True), 0, [])]
    all_to_all x0 -> x1, starting transfers between devices: none -> 8.76 us  [rows_first(): lax.all_to_all(jnp.stack([both] * lax.axis_size(axis)), axis, 0, 0)]
    another operation x0 -> x1, local copies, waits for them, and re-layouts: none -> 5.56 us  [rows_first(): jnp.stack([both] * lax.axis_size(axis))]
where the time goes in v1:
time: 253 us; the launch traced here: 252 us
  waiting for transfers between devices  161 us (64%)
  blocking collectives  53.3 us (21%)
  matrix products  13.9 us (5%)
  local copies, waits for them, and re-layouts  9.05 us (4%)
  starting transfers between devices  8.76 us (3%)
  other arithmetic  6.13 us (2%)
    all_to_all x1, waiting for transfers between devices, rows_first(): lax.all_to_all(jnp.stack([both] * lax.axis_size(axis)), axis, 0, 0)  161 us
    all_gather x4, blocking collectives, collected_together(): both, at, found = (lax.all_gather(jnp.concatenate(lines), axis), 0, {})  53.3 us
    all_to_all x1, starting transfers between devices, rows_first(): lax.all_to_all(jnp.stack([both] * lax.axis_size(axis)), axis, 0, 0)  8.76 us
    dot_general x1, matrix products, body(): jnp.dot(ref_full, ref_unembed, preferred_element_type=jnp.float32)  7.55 us
    dot_general x1, matrix products, body(): jnp.dot(policy_full, policy_unembed, preferred_element_type=jnp.float32)  6.35 us
    another operation x1, local copies, waits for them, and re-layouts, rows_first(): jnp.stack([both] * lax.axis_size(axis))  5.56 us
  transfers between devices with their start and end apart: 1, of which 1 were waited for; matrix products, arithmetic and copies ran while one was open for 0% of the time, Pallas kernels for 0%

profile of v1, /device:TPU:1, one launch (start us, length us, event | category | flops | bytes accessed | tf_op | source)
XLA Modules:
  0.0 252.4 jit_solution(15345800456918349386)
XLA Ops:
  0.0 1.6 pad_maximum_fusion
  1.6 5.6 %stack.2 = bf16[8,448,2048]{2,1,0:T(8,128)(2,1)} broadcast(bf16[448,2048]{1,0:T(8,128)(2,1)S(1)} %pad_maximum_fusion), dimensions={1,2} | broadcast | bytes 16515072 | tf_op jit(solution)/shard_map/stack | solution.py:16
  7.2 0.0 copy-start
  7.2 8.8 %all-to-all-start = ((bf16[8,448,2048]{2,1,0:T(8,128)(2,1)}), bf16[8,448,2048]{2,1,0:T(8,128)(2,1)}, u32[]{:S(2)}, u32[]{:S(2)}) async-start(bf16[8,448,2048]{2,1,0:T(8,128)(2,1)} %stack.2), calls=%async_computation | async-start | bytes 29360128 | tf_op jit(solution)/shard_map/all_to_all | solution.py:16
  16.0 0.0 copy-done
  16.0 0.0 copy-done.1
  16.0 161.1 %all-to-all-done = bf16[8,448,2048]{2,1,0:T(8,128)(2,1)} async-done(((bf16[8,448,2048]{2,1,0:T(8,128)(2,1)}), bf16[8,448,2048]{2,1,0:T(8,128)(2,1)}, u32[]{:S(2)}, u32[]{:S(2)}) %all-to-all-start) | async-done | bytes 14680096 | tf_op jit(solution)/shard_map/all_to_all | solution.py:16
  177.1 7.5 %fusion = f32[1024,512]{0,1:T(8,128)S(1)} fusion(bf16[3584,512]{1,0:T(8,128)(2,1)} %param.11, bf16[3584,2048]{1,0:T(8,128)(2,1)} %bitcast.2), kind=kOutput, calls=%fused_computation | convolution fusion | flops 3758096384 | bytes 13107200 | tf_op jit(solution)/shard_map/dot_general | solution.py:63
  184.7 0.0 copy-done.2
  184.7 6.4 %fusion.62 = (f32[1024]{0:T(1024)S(1)}, f32[1024,512]{0,1:T(8,128)S(1)}) fusion(f32[1024,512]{0,1:T(8,128)S(1)} %fusion, f32[1024]{0:T(1024)S(1)} %get-tuple-element.14, bf16[3584,512]{1,0:T(8,128)(2,1)S(1)} %copy-done.2, bf16[3584,2048]{1,0:T(8,128)(2,1)} %bitcast.2, f32[1024]{0:T(1024)S(1)} %get-tuple-element.13), kind=kOutput, calls=%fused_computation.100 | convolution fusion | flops 3760192512 | bytes 15216640 | tf_op jit(solution)/shard_map/dot_general | solution.py:62
  191.1 0.3 exponential_reduce_fusion
  191.4 20.2 %all-gather = f32[16384,1]{0,1:T(1,128)S(1)} all-gather(f32[2048,1]{0,1:T(1,128)S(1)} %pad_maximum_fusion.1), channel_id=2, replica_groups=mesh['vrow_0'=8,'vrow_1'=4,'vcol_0'=4,'vcol_1'=2] {'vrow_0'}, dimensions={0}, use_global_device_ids=true | all-gather | bytes 73728 | tf_op jit(solution)/shard_map/all_gather | solution.py:36
  211.7 0.1 fusion.25
  211.8 9.5 %all-gather.1 = f32[8192,1]{0,1:T(1,128)S(1)} all-gather(f32[2048,1]{0,1:T(1,128)S(1)} %pad_maximum_fusion.2), channel_id=3, replica_groups=mesh['vrow_0'=8,'vrow_1'=4,'vcol_0'=4,'vcol_1'=2] {'vrow_1'}, dimensions={0}, use_global_device_ids=true | all-gather | bytes 40960 | tf_op jit(solution)/shard_map/all_gather | solution.py:36
  221.3 0.5 broadcast.18
  221.8 0.7 reduce.12
  222.6 0.1 fusion.16
  222.7 9.0 %all-gather.2 = f32[8192,1]{0,1:T(1,128)S(1)} all-gather(f32[2048,1]{0,1:T(1,128)S(1)} %pad_maximum_fusion.3), channel_id=4, replica_groups=mesh['vrow_0'=8,'vrow_1'=4,'vcol_0'=4,'vcol_1'=2] {'vcol_0'}, dimensions={0}, use_global_device_ids=true | all-gather | bytes 40960 | tf_op jit(solution)/shard_map/all_gather | solution.py:36
  231.7 0.7 reduce.13
  232.5 0.1 fusion.7
  232.5 14.5 %all-gather.3 = f32[4096,1]{0,1:T(1,128)S(1)} all-gather(f32[2048,1]{0,1:T(1,128)S(1)} %pad_maximum_fusion.4), channel_id=5, replica_groups=mesh['vrow_0'=8,'vrow_1'=4,'vcol_0'=4,'vcol_1'=2] {'vcol_1'}, dimensions={0}, use_global_device_ids=true | all-gather | bytes 24576 | tf_op jit(solution)/shard_map/all_gather | solution.py:36
  247.0 0.7 reduce.14
  247.8 1.8 subtract_subtract_fusion
  249.6 2.9 %copy.8 = f32[1024,512]{1,0:T(8,128)} copy(f32[1024,512]{0,1:T(8,128)} %subtract_subtract_fusion) | data formatting | bytes 4194304 | tf_op jit(solution)/shard_map/sub | solution.py:69
  (13 shorter events, 0.2 us)
Async XLA Ops:
  7.2 8.8 %copy-start = (s32[1024]{0:T(1024)S(1)}, s32[1024]{0:T(1024)}, u32[]{:S(2)}) copy-start(s32[1024]{0:T(1024)} %param.9) | copy-start | bytes 12292
  7.2 8.8 %copy-start.1 = (s32[1024]{0:T(1024)S(1)}, s32[1024]{0:T(1024)}, u32[]{:S(2)}) copy-start(s32[1024]{0:T(1024)} %param.8) | copy-start | bytes 12292
  7.2 169.9 %all-to-all-start = ((bf16[8,448,2048]{2,1,0:T(8,128)(2,1)}), bf16[8,448,2048]{2,1,0:T(8,128)(2,1)}, u32[]{:S(2)}, u32[]{:S(2)}) async-start(bf16[8,448,2048]{2,1,0:T(8,128)(2,1)} %stack.2), calls=%async_computation | async-start | bytes 29360128 | tf_op jit(solution)/shard_map/all_to_all | solution.py:16
  177.1 7.6 %copy-start.2 = (bf16[3584,512]{1,0:T(8,128)(2,1)S(1)}, bf16[3584,512]{1,0:T(8,128)(2,1)}, u32[]{:S(2)}) copy-start(bf16[3584,512]{1,0:T(8,128)(2,1)} %param.10) | copy-start | bytes 11010052
